TPU v7x, 32 devices: a whole 2x2x4 slice. The times are simulated.
32 devices in a mesh: seq: 2 (over x), tensor: 4 (over z), bucket: 4 (over y, core).
Axes of the slice: x: 2, y: 2, z: 4, core: 2. Of those that a mesh axis runs over, the one named last changes fastest.
Arguments:
- queries: bfloat16 [4, 1024, 3072], P('bucket', ('seq', 'tensor')), may hold values from -6 to 6
- keys: bfloat16 [4, 1024, 3072], P('bucket', ('seq', 'tensor')), may hold values from -6 to 6
- values: bfloat16 [4, 1024, 3072], P('bucket', ('seq', 'tensor')), may hold values from -6 to 6
- lengths: int32 [4], P('bucket'), may hold values from 256 to 1024, as said below
- out_weight: bfloat16 [3072, 3072], P(('seq', 'bucket'), 'tensor'), may hold values from -0.109375 to 0.109375
Outputs:
- projected: bfloat16 [4, 1024, 3072], P('bucket', ('seq', 'tensor'))
Inputs may be any that keep to these rules, and one draw needn't show every extreme that they name: `lengths`: each bucket has 256 to 1024 live tokens, and at least one bucket has all 1024.
All inputs are finite; a program needn't handle non-finite values.
Results may differ from a plain program's by a relative error of at most 0.018.
Values may be sent and summed in bfloat16 or wider, within the bound.
A program may use at most 128 MiB of HBM per device.

v0:
```python
import functools
import math

import jax
import jax.numpy as jnp
from jax import lax
from jax.experimental import pallas as pl
from jax.experimental.pallas import tpu as pltpu
from jax.sharding import PartitionSpec as P

HS = 128


MASKED_SCORE = -1e30


def shards(queries, keys, values, lengths, out_weight):
    tok_rows = queries.shape[1]
    n_tensor = lax.axis_size("tensor")
    tensor_index = lax.axis_index("tensor")
    live_len = lengths[0]
    local_q, local_k, local_v = (
        lax.all_to_all(queries[0], "seq", split_axis=1, concat_axis=0, tiled=True),
        lax.all_to_all(keys[0], "seq", split_axis=1, concat_axis=0, tiled=True),
        lax.all_to_all(values[0], "seq", split_axis=1, concat_axis=0, tiled=True),
    )
    row_count, col_count = local_q.shape
    head_count = col_count // HS
    query_heads = local_q.reshape(row_count, head_count, HS)

    def spots(first_row, total_rows):
        index_row = first_row + jnp.arange(total_rows, dtype=jnp.int32)
        owner = index_row // row_count
        within = index_row % row_count
        return (within // tok_rows * n_tensor + owner) * tok_rows + within % tok_rows

    query_usable = spots(tensor_index * row_count, row_count) < live_len
    initial = (
        jnp.full((row_count, head_count), MASKED_SCORE, jnp.float32),
        jnp.zeros((row_count, head_count), jnp.float32),
        jnp.zeros((row_count, head_count, HS), jnp.float32),
    )
    carried = initial
    first_row = jnp.int32(0)
    key_rows = lax.all_gather(local_k, "tensor", axis=0, tiled=True)
    value_rows = lax.all_gather(local_v, "tensor", axis=0, tiled=True)
    for offset in range(key_rows.shape[0] // row_count):
        row_peak, row_sum, accumulated = carried
        key_tile = key_rows[offset * row_count : (offset + 1) * row_count].reshape(
            row_count, head_count, HS
        )
        value_tile = value_rows[offset * row_count : (offset + 1) * row_count].reshape(
            row_count, head_count, HS
        )
        key_usable = spots(first_row + offset * row_count, row_count) < live_len
        scores = jnp.einsum(
            "qhd,khd->qhk", query_heads, key_tile, preferred_element_type=jnp.float32
        ) * HS ** (-0.5)
        scores = jnp.where(key_usable[None, None, :], scores, MASKED_SCORE)
        peak_new = jnp.maximum(row_peak, jnp.max(scores, axis=-1))
        exponent = jnp.where(key_usable[None, None, :], jnp.exp(scores - peak_new[..., None]), 0.0)
        rescale = jnp.exp(row_peak - peak_new)
        accumulated = accumulated * rescale[..., None] + jnp.einsum(
            "qhk,khd->qhd",
            exponent.astype(jnp.bfloat16),
            value_tile,
            preferred_element_type=jnp.float32,
        )
        carried = (peak_new, row_sum * rescale + jnp.sum(exponent, axis=-1), accumulated)
    row_peak, row_sum, accumulated = carried
    attended = accumulated / row_sum[..., None]
    mixed = jnp.where(query_usable[:, None], attended.reshape(row_count, col_count), 0.0).astype(
        jnp.bfloat16
    )
    restored = lax.all_to_all(mixed, "seq", split_axis=0, concat_axis=1, tiled=True)
    wide_weight = lax.all_gather(out_weight, "tensor", axis=1, tiled=True)
    summed = jnp.dot(
        restored,
        lax.all_gather(wide_weight, ("seq", "bucket"), axis=0, tiled=True),
        preferred_element_type=jnp.float32,
    )
    return summed.astype(jnp.bfloat16)[None]


def whole_kernel(
    axes, sizes, len_ref, q_ref, k_ref, v_ref, w_ref, out_ref,
    got, done, mixed, weight, part_out, part_in, own_part,
    qkv_send, qkv_recv, att_send, att_recv, up_send, down_send, line_recv,
    far_send, far_recv, near_send, near_recv, part_send, part_recv, out_sem,
):
    n_seq, n_tensor, n_bucket = sizes
    s, t, b = lax.axis_index("seq"), lax.axis_index("tensor"), lax.axis_index("bucket")
    group = n_seq * n_tensor
    rows = q_ref.shape[1]
    width = q_ref.shape[2]
    heads = width // HS // group
    w_rows, w_cols = w_ref.shape
    block = n_seq * rows
    live = len_ref[0]

    def device(ds, dt, db):
        place = {"seq": ds, "tensor": dt, "bucket": db}
        return tuple(place[name] for name in axes)

    def remote(src, dst, send, recv, where):
        return pltpu.make_async_remote_copy(
            src_ref=src, dst_ref=dst, send_sem=send, recv_sem=recv,
            device_id=where, device_id_type=pl.DeviceIdType.MESH,
        )

    me = s * n_tensor + t
    streams = (q_ref, k_ref, v_ref)

    def spot(ds, dt):
        return pl.ds(pl.multiple_of((dt * n_seq + ds) * rows, rows), rows)

    def qkv_copy(h, j, step, peer, source):
        cols = pl.ds(pl.multiple_of((peer * heads + h) * HS, HS), HS)
        return remote(
            streams[j].at[0, :, cols],
            got.at[h, j, spot(source // n_tensor, source % n_tensor), :],
            qkv_send.at[h, j, step],
            qkv_recv.at[h, j, step],
            device(peer // n_tensor, peer % n_tensor, b),
        )

    def start_qkv(h):
        def body(step, carry):
            peer = (me + step) % group
            for j in range(3):
                qkv_copy(h, j, step, peer, me).start()
            return carry

        lax.fori_loop(1, group, body, 0)

    def piece(row_block, col_block):
        return weight.at[
            pl.ds(pl.multiple_of(row_block * w_rows, w_rows), w_rows),
            pl.ds(pl.multiple_of(col_block * w_cols, w_cols), w_cols),
        ]

    far, near = (b + 2) % 4, b + 1 - 2 * (b % 2)

    def up_copy(p):
        return remote(piece(b, p), piece(b, p), up_send.at[p], line_recv.at[p], device(s, t + 1, b))

    def down_copy(p):
        return remote(piece(b, p), piece(b, p), down_send.at[p], line_recv.at[p], device(s, t - 1, b))

    def far_copy(p, row_block):
        return remote(piece(row_block, p), piece(row_block, p), far_send.at[p], far_recv.at[p], device(s, t, far))

    def near_copy(k, p, row_block):
        return remote(
            piece(row_block, p), piece(row_block, p), near_send.at[k, p], near_recv.at[k, p], device(s, t, near)
        )

    def spread(p):
        far_copy(p, b).start()
        near_copy(0, p, b).start()

    def relay(k):
        @pl.when(t >= k)
        def _():
            up_copy(t - k).wait_recv()

            @pl.when(t < n_tensor - 1)
            def _():
                up_copy(t - k).start()

            spread(t - k)

        @pl.when(t + k < n_tensor)
        def _():
            down_copy(t + k).wait_recv()

            @pl.when(t > 0)
            def _():
                down_copy(t + k).start()

            spread(t + k)

    weight[
        pl.ds(pl.multiple_of(b * w_rows, w_rows), w_rows),
        pl.ds(pl.multiple_of(t * w_cols, w_cols), w_cols),
    ] = w_ref[...]

    @pl.when(t < n_tensor - 1)
    def _():
        up_copy(t).start()

    @pl.when(t > 0)
    def _():
        down_copy(t).start()

    start_qkv(0)
    spread(t)

    for h in range(heads):
        cols = pl.ds(pl.multiple_of((me * heads + h) * HS, HS), HS)
        for j in range(3):
            got[h, j, spot(s, t), :] = streams[j][0, :, cols]

    total = group * rows
    index = lax.broadcasted_iota(jnp.int32, (1, total), 1)
    token = (index % block // rows * n_tensor + index // block) * rows + index % rows
    usable = token < live
    factor = HS ** (-0.5) * math.log2(math.e)

    def slot_of(side):
        return (side + s) % 2

    def att_copy(h, step, target, source, side=None):
        first, count, slot = (0, block, 0) if side is None else (side * rows, rows, slot_of(side))
        here = pl.ds(pl.multiple_of(target * block + first, rows), count)
        there = pl.ds(pl.multiple_of(first, rows), count)
        cols = pl.ds(pl.multiple_of((source * heads + h) * HS, HS), HS)
        return remote(
            done.at[h, here, :], mixed.at[there, cols],
            att_send.at[h, slot, step], att_recv.at[h, slot, step], device(s, target, b),
        )

    def attend(h, target, first, count):
        here = pl.ds(pl.multiple_of(target * block + first, rows), count)
        row = first + lax.broadcasted_iota(jnp.int32, (count, 1), 0)
        return attend_rows(h, got[h, 0, here, :], (row // rows * n_tensor + target) * rows + row % rows)

    def attend_rows(h, query, own_token):
        scores = lax.dot_general(
            query, got[h, 1], (((1,), (1,)), ((), ())), preferred_element_type=jnp.float32
        )
        scores = jnp.where(usable, scores, MASKED_SCORE)
        peak = jnp.max(scores, axis=-1, keepdims=True)
        expo = jnp.exp2((scores - peak) * factor)
        denominator = jnp.sum(expo, axis=-1, keepdims=True)
        result = jnp.dot(expo.astype(jnp.bfloat16), got[h, 2], preferred_element_type=jnp.float32) / denominator
        return jnp.where(own_token < live, result, 0.0).astype(jnp.bfloat16)

    def attend_all(h, first, count, side):
        def one(step, carry):
            target = (t + step) % n_tensor
            done[h, pl.ds(pl.multiple_of(target * block + first, rows), count), :] = attend(h, target, first, count)
            att_copy(h, step, target, t, side).start()
            return carry

        lax.fori_loop(1, n_tensor, one, 0)
        mixed[
            pl.ds(pl.multiple_of(first, rows), count), pl.ds(pl.multiple_of((t * heads + h) * HS, HS), HS)
        ] = attend(h, t, first, count)

    def attend_side(h, side):
        row = lax.broadcasted_iota(jnp.int32, (rows, 1), 0)
        for step in range(0, n_tensor, 2):
            targets = [(t + step + i) % n_tensor for i in (1, 2)]
            spans = [pl.ds(pl.multiple_of(target * block + side * rows, rows), rows) for target in targets]
            result = attend_rows(
                h,
                jnp.concatenate([got[h, 0, span, :] for span in spans], axis=0),
                jnp.concatenate([(side * n_tensor + target) * rows + row for target in targets], axis=0),
            )
            for i in range(2):
                if step + i + 1 < n_tensor:
                    done[h, spans[i], :] = result[i * rows : (i + 1) * rows]
                    att_copy(h, step + i + 1, targets[i], t, side).start()
                else:
                    mixed[
                        pl.ds(pl.multiple_of(side * rows, rows), rows),
                        pl.ds(pl.multiple_of((t * heads + h) * HS, HS), HS),
                    ] = result[i * rows : (i + 1) * rows]

    upper = t // 2
    order = (t, 1 - t + 4 * upper, 2 - upper, 3 - 3 * upper)

    def forward(p):
        far_copy(p, far).wait_recv()
        near_copy(1, p, far).start()

    for h in range(heads):
        if h == 0:
            relay(1)
            for later in range(1, heads):
                start_qkv(later)
        elif h == 1:
            relay(2)

        def arrive(step, carry):
            source = (me + group - step) % group
            for j in range(3):
                qkv_copy(h, j, step, me, source).wait_recv()
            return carry

        lax.fori_loop(1, group, arrive, 0)
        if 1 <= h <= 2:
            forward(order[h - 1])
        if h + 1 < heads:
            attend_all(h, 0, block, None)
        else:
            attend_side(h, 1 - s)
            attend_side(h, s)
    for k in range(heads, 3):
        relay(k)
    for k in range(max(heads - 1, 0), 3):
        forward(order[k])

    def back(h, side):
        def body(step, carry):
            att_copy(h, step, t, (t + n_tensor - step) % n_tensor, side).wait_recv()
            return carry

        lax.fori_loop(1, n_tensor, body, 0)

    def cut_of(p):
        return pl.ds(pl.multiple_of(p * w_cols, w_cols), w_cols)

    def part_copy(p):
        cut = cut_of(p)
        return remote(
            part_out.at[:, cut], part_in.at[:, cut], part_send.at[p], part_recv.at[p], device(1 - s, t, b)
        )

    def leave(p):
        cut = cut_of(p)
        return pltpu.make_async_copy(part_in.at[:, cut], out_ref.at[0, :, cut], out_sem.at[p])

    for h in range(heads - 1):
        back(h, None)
    back(heads - 1, 1 - s)
    for k, p in enumerate(order):
        near_copy(0, p, near).wait_recv()
        near_copy(1, p, (near + 2) % 4).wait_recv()
        cut = cut_of(p)
        part_out[:, cut] = jnp.dot(
            mixed[pl.ds(pl.multiple_of((1 - s) * rows, rows), rows), :], weight[:, cut],
            preferred_element_type=jnp.float32,
        ).astype(jnp.bfloat16)
        part_copy(p).start()
        if k == 0:
            relay(3)
        if k == 2:
            forward(order[3])
    back(heads - 1, s)
    for p in order:
        cut = cut_of(p)
        own_part[:, cut] = jnp.dot(
            mixed[pl.ds(pl.multiple_of(s * rows, rows), rows), :], weight[:, cut],
            preferred_element_type=jnp.float32,
        )
    for p in order:
        cut = cut_of(p)
        part_copy(p).wait_recv()
        part_in[:, cut] = (own_part[:, cut] + part_in[:, cut].astype(jnp.float32)).astype(jnp.bfloat16)
        leave(p).start()

    for h in range(heads):
        def sent(step, carry):
            peer = (me + step) % group
            for j in range(3):
                qkv_copy(h, j, step, peer, me).wait_send()
            return carry

        lax.fori_loop(1, group, sent, 0)

        def att_sent(step, carry):
            if h + 1 < heads:
                att_copy(h, step, (t + step) % n_tensor, t).wait_send()
            else:
                att_copy(h, step, (t + step) % n_tensor, t, 1 - s).wait_send()
                att_copy(h, step, (t + step) % n_tensor, t, s).wait_send()
            return carry

        lax.fori_loop(1, n_tensor, att_sent, 0)
    for k in range(n_tensor):
        @pl.when((t >= k) & (t < n_tensor - 1))
        def _():
            up_copy(t - k).wait_send()

        @pl.when((t + k < n_tensor) & (t > 0))
        def _():
            down_copy(t + k).wait_send()

    for p in range(n_tensor):
        far_copy(p, b).wait_send()
        near_copy(0, p, b).wait_send()
        near_copy(1, p, far).wait_send()
        part_copy(p).wait_send()
        leave(p).wait()


def fused(axes, sizes, queries, keys, values, lengths, out_weight):
    n_seq, n_tensor, n_bucket = sizes
    rows, width = queries.shape[1:]
    group = n_seq * n_tensor
    heads = width // HS // group
    total = group * rows
    half = width // n_seq
    vmem = pl.BlockSpec(memory_space=pltpu.VMEM)
    dma = pltpu.SemaphoreType.DMA
    return pl.pallas_call(
        functools.partial(whole_kernel, axes, sizes),
        out_shape=jax.ShapeDtypeStruct(queries.shape, queries.dtype),
        in_specs=[pl.BlockSpec(memory_space=pltpu.SMEM), vmem, vmem, vmem, vmem],
        out_specs=pl.BlockSpec(memory_space=pl.ANY),
        scratch_shapes=[
            pltpu.VMEM((heads, 3, total, HS), jnp.bfloat16),
            pltpu.VMEM((heads, total, HS), jnp.bfloat16),
            pltpu.VMEM((n_seq * rows, half), jnp.bfloat16),
            pltpu.VMEM((half, width), jnp.bfloat16),
            pltpu.VMEM((rows, width), jnp.bfloat16),
            pltpu.VMEM((rows, width), jnp.bfloat16),
            pltpu.VMEM((rows, width), jnp.float32),
            dma((heads, 3, group)),
            dma((heads, 3, group)),
            dma((heads, 2, n_tensor)),
            dma((heads, 2, n_tensor)),
            dma((n_tensor,)),
            dma((n_tensor,)),
            dma((n_tensor,)),
            dma((n_tensor,)),
            dma((n_tensor,)),
            dma((2, n_tensor)),
            dma((2, n_tensor)),
            dma((n_tensor,)),
            dma((n_tensor,)),
            dma((n_tensor,)),
        ],
        compiler_params=pltpu.CompilerParams(has_side_effects=True, vmem_limit_bytes=56 * 1024 * 1024),
    )(lengths, queries, keys, values, out_weight)


def solution(mesh):
    in_specs = (
        P("bucket", ("seq", "tensor"), None),
        P("bucket", ("seq", "tensor"), None),
        P("bucket", ("seq", "tensor"), None),
        P("bucket"),
        P(("seq", "bucket"), "tensor"),
    )
    out_specs = P("bucket", ("seq", "tensor"), None)
    sizes = tuple(mesh.shape[name] for name in ("seq", "tensor", "bucket"))

    def step(queries, keys, values, lengths, out_weight):
        head_count = queries.shape[2] // HS
        fits = sizes[0] == 2 and sizes[1] == sizes[2] == 4 and head_count % (sizes[0] * sizes[1]) == 0
        if fits:
            return fused(mesh.axis_names, sizes, queries, keys, values, lengths, out_weight)
        return shards(queries, keys, values, lengths, out_weight)

    return jax.shard_map(step, mesh=mesh, in_specs=in_specs, out_specs=out_specs, check_vma=False)
```

profile of v0, /device:TPU:0, one launch (start us, length us, event | category | flops | bytes accessed | tf_op | source)
XLA Modules:
  0.0 131.0 jit_solution(6324172747448554304)
XLA Ops:
  0.7 128.3 %shard_map.55 = bf16[1,128,3072]{2,1,0:T(8,128)(2,1)} custom-call(s32[1]{0:T(128)S(6)} %copy.7.len_ref, bf16[1,128,3072]{2,1,0:T(8,128)(2,1)} %q_ref.1, bf16[1,128,3072]{2,1,0:T(8,128)(2,1)} %k_ref.1, bf16[1,128,3072]{2,1,0:T(8,128)(2,1)} %v_ref.1, bf16[384,768]{1,0:T(8,128)(2,1)} %w_ref.1), custom_call_target="tpu_custom_call" | custom-call | tf_op jit(solution)/shard_map/pallas_call | solution.py:398
  128.9 2.1 %copy.8 = bf16[1,128,3072]{2,1,0:T(8,128)(2,1)} copy(bf16[1,128,3072]{2,1,0:T(8,128)(2,1)} %shard_map.55) | data formatting | bytes 1572864
where the time goes:
time: 132 us; the launch traced here: 131 us
  Pallas kernels  128 us (97%)
  local copies, waits for them, and re-layouts  2.06 us (2%)
    pallas_call x1, Pallas kernels, fused(): pl.pallas_call(functools.partial(whole_kernel, axes, sizes), out_shape=ja...  128 us

commit v1 on v0

v1 whole, which is shorter than its diff:
```python
import functools
import math

import jax
import jax.numpy as jnp
from jax import lax
from jax.experimental import pallas as pl
from jax.experimental.pallas import tpu as pltpu
from jax.sharding import PartitionSpec as P

HS = 128


MASKED_SCORE = -1e30


CHUNKS = 2


def shards(queries, keys, values, lengths, out_weight):
    tok_rows = queries.shape[1]
    n_tensor = lax.axis_size("tensor")
    tensor_index = lax.axis_index("tensor")
    live_len = lengths[0]
    local_q, local_k, local_v = (
        lax.all_to_all(queries[0], "seq", split_axis=1, concat_axis=0, tiled=True),
        lax.all_to_all(keys[0], "seq", split_axis=1, concat_axis=0, tiled=True),
        lax.all_to_all(values[0], "seq", split_axis=1, concat_axis=0, tiled=True),
    )
    row_count, col_count = local_q.shape
    head_count = col_count // HS
    query_heads = local_q.reshape(row_count, head_count, HS)

    def spots(first_row, total_rows):
        index_row = first_row + jnp.arange(total_rows, dtype=jnp.int32)
        owner = index_row // row_count
        within = index_row % row_count
        return (within // tok_rows * n_tensor + owner) * tok_rows + within % tok_rows

    query_usable = spots(tensor_index * row_count, row_count) < live_len
    initial = (
        jnp.full((row_count, head_count), MASKED_SCORE, jnp.float32),
        jnp.zeros((row_count, head_count), jnp.float32),
        jnp.zeros((row_count, head_count, HS), jnp.float32),
    )
    carried = initial
    first_row = jnp.int32(0)
    key_rows = lax.all_gather(local_k, "tensor", axis=0, tiled=True)
    value_rows = lax.all_gather(local_v, "tensor", axis=0, tiled=True)
    for offset in range(key_rows.shape[0] // row_count):
        row_peak, row_sum, accumulated = carried
        key_tile = key_rows[offset * row_count : (offset + 1) * row_count].reshape(
            row_count, head_count, HS
        )
        value_tile = value_rows[offset * row_count : (offset + 1) * row_count].reshape(
            row_count, head_count, HS
        )
        key_usable = spots(first_row + offset * row_count, row_count) < live_len
        scores = jnp.einsum(
            "qhd,khd->qhk", query_heads, key_tile, preferred_element_type=jnp.float32
        ) * HS ** (-0.5)
        scores = jnp.where(key_usable[None, None, :], scores, MASKED_SCORE)
        peak_new = jnp.maximum(row_peak, jnp.max(scores, axis=-1))
        exponent = jnp.where(key_usable[None, None, :], jnp.exp(scores - peak_new[..., None]), 0.0)
        rescale = jnp.exp(row_peak - peak_new)
        accumulated = accumulated * rescale[..., None] + jnp.einsum(
            "qhk,khd->qhd",
            exponent.astype(jnp.bfloat16),
            value_tile,
            preferred_element_type=jnp.float32,
        )
        carried = (peak_new, row_sum * rescale + jnp.sum(exponent, axis=-1), accumulated)
    row_peak, row_sum, accumulated = carried
    attended = accumulated / row_sum[..., None]
    mixed = jnp.where(query_usable[:, None], attended.reshape(row_count, col_count), 0.0).astype(
        jnp.bfloat16
    )
    restored = lax.all_to_all(mixed, "seq", split_axis=0, concat_axis=1, tiled=True)
    wide_weight = lax.all_gather(out_weight, "tensor", axis=1, tiled=True)
    summed = jnp.dot(
        restored,
        lax.all_gather(wide_weight, ("seq", "bucket"), axis=0, tiled=True),
        preferred_element_type=jnp.float32,
    )
    return summed.astype(jnp.bfloat16)[None]


def whole_kernel(
    axes, sizes, len_ref, q_ref, k_ref, v_ref, w_ref, out_ref,
    held, got, done, mixed, weight, part_out, part_in, own_part, load_sem, own_sem,
    qkv_send, qkv_recv, att_send, att_recv, up_send, down_send, line_recv,
    far_send, far_recv, near_send, near_recv, part_send, part_recv, out_sem,
):
    n_seq, n_tensor, n_bucket = sizes
    s, t, b = lax.axis_index("seq"), lax.axis_index("tensor"), lax.axis_index("bucket")
    group = n_seq * n_tensor
    rows = q_ref.shape[1]
    width = q_ref.shape[2]
    heads = width // HS // group
    w_rows, w_cols = w_ref.shape
    live = len_ref[0]

    def device(ds, dt, db):
        place = {"seq": ds, "tensor": dt, "bucket": db}
        return tuple(place[name] for name in axes)

    def remote(src, dst, send, recv, where):
        return pltpu.make_async_remote_copy(
            src_ref=src, dst_ref=dst, send_sem=send, recv_sem=recv,
            device_id=where, device_id_type=pl.DeviceIdType.MESH,
        )

    me = s * n_tensor + t
    streams = (q_ref, k_ref, v_ref)
    barrier = pltpu.get_barrier_semaphore()

    def spot(place):
        return pl.ds(pl.multiple_of(place * rows, rows), rows)

    def peer_of(e):
        return (s + e // n_tensor) % 2, (t + e % n_tensor) % n_tensor

    def source_of(e):
        return (s + e // n_tensor) % 2, (t + n_tensor - e % n_tensor) % n_tensor

    def qkv_copy(h, j, e, to, source):
        cols = pl.ds(pl.multiple_of(((to[0] * n_tensor + to[1]) * heads + h) * HS, HS), HS)
        return remote(
            held.at[j, :, cols],
            got.at[h, j, spot(source[0] * n_tensor + source[1]), :],
            qkv_send.at[h, j, e],
            qkv_recv.at[h, j, e],
            device(to[0], to[1], b),
        )

    def start_stream(h, js, first, last):
        def body(e, carry):
            for j in js:
                qkv_copy(h, j, e, peer_of(e), (s, t)).start()
            return carry

        lax.fori_loop(first, last, body, 0)

    def arrive(h, js, first, last):
        def body(e, carry):
            for j in js:
                qkv_copy(h, j, e, (s, t), source_of(e)).wait_recv()
            return carry

        lax.fori_loop(first, last, body, 0)

    def own_arrive(h):
        for j in range(3):
            own_copy(h, j).wait()

    def start_across(h):
        start_stream(h, (1, 2, 0), n_tensor, n_tensor + 1)

    def start_kv_far(h, first=1, last=4):
        start_stream(h, (1, 2), first, last)
        start_stream(h, (1, 2, 0), n_tensor + first, n_tensor + last)


    def start_own(h):
        start_stream(h, (0,), 1, n_tensor)

    chunk = w_rows // CHUNKS

    def piece(row_block, col_block, c):
        return weight.at[
            pl.ds(pl.multiple_of(row_block * w_rows + c * chunk, chunk), chunk),
            pl.ds(pl.multiple_of(col_block * w_cols, w_cols), w_cols),
        ]

    far, near = (b + 2) % 4, b + 1 - 2 * (b % 2)

    def up_copy(p, c):
        return remote(
            piece(b, p, c), piece(b, p, c), up_send.at[p, c], line_recv.at[p, c], device(s, t + 1, b)
        )

    def down_copy(p, c):
        return remote(
            piece(b, p, c), piece(b, p, c), down_send.at[p, c], line_recv.at[p, c], device(s, t - 1, b)
        )

    def far_copy(p, c, row_block):
        return remote(
            piece(row_block, p, c), piece(row_block, p, c), far_send.at[p, c], far_recv.at[p, c], device(s, t, far)
        )

    def near_copy(k, p, c, row_block):
        return remote(
            piece(row_block, p, c), piece(row_block, p, c),
            near_send.at[k, p, c], near_recv.at[k, p, c], device(s, t, near),
        )

    def spread(p, c):
        far_copy(p, c, b).start()
        near_copy(0, p, c, b).start()

    def relay_chunk(k, c):
        @pl.when(t >= k)
        def _():
            up_copy(t - k, c).wait_recv()

            @pl.when(t < n_tensor - 1)
            def _():
                up_copy(t - k, c).start()

            spread(t - k, c)

        @pl.when(t + k < n_tensor)
        def _():
            down_copy(t + k, c).wait_recv()

            @pl.when(t > 0)
            def _():
                down_copy(t + k, c).start()

            spread(t + k, c)

    def relay(k):
        for c in range(CHUNKS):
            relay_chunk(k, c)

    own_piece = weight.at[
        pl.ds(pl.multiple_of(b * w_rows, w_rows), w_rows),
        pl.ds(pl.multiple_of(t * w_cols, w_cols), w_cols),
    ]
    weight_load = pltpu.make_async_copy(w_ref, own_piece, load_sem.at[3])
    weight_load.start()

    def load(j):
        return pltpu.make_async_copy(streams[j].at[0], held.at[j], load_sem.at[j])

    def own_copy(h, j):
        cols = pl.ds(pl.multiple_of((me * heads + h) * HS, HS), HS)
        return pltpu.make_async_copy(streams[j].at[0, :, cols], got.at[h, j, spot(me), :], own_sem.at[h, j])

    def greet(where):
        pl.semaphore_signal(barrier, inc=1, device_id=where, device_id_type=pl.DeviceIdType.MESH)

    for e in range(1, group):
        to = peer_of(e)
        greet(device(to[0], to[1], b))
    greet(device(s, t, far))
    greet(device(s, t, near))
    for j in (1, 2, 0):
        load(j).start()
    for h in range(heads):
        for j in range(3):
            own_copy(h, j).start()
    pl.semaphore_wait(barrier, group + 1)
    weight_load.wait()

    for c in range(CHUNKS):
        @pl.when(t < n_tensor - 1)
        def _():
            up_copy(t, c).start()

        @pl.when(t > 0)
        def _():
            down_copy(t, c).start()

        spread(t, c)
    for j in (1, 2, 0):
        load(j).wait()

    upper = t // 2
    order = (t, 1 - t + 4 * upper, 2 - upper, 3 - 3 * upper)

    def forward(p):
        for c in range(CHUNKS):
            far_copy(p, c, far).wait_recv()
            near_copy(1, p, c, far).start()

    total = group * rows
    usable = lax.broadcasted_iota(jnp.int32, (1, total), 1) < live
    factor = HS ** (-0.5) * math.log2(math.e)

    def att_copy(h, f, d, target, source):
        cols = pl.ds(pl.multiple_of((source * heads + h) * HS, HS), HS)
        return remote(
            done.at[h, spot((s + f) % 2 * n_tensor + target), :], mixed.at[f, :, cols],
            att_send.at[h, f, d], att_recv.at[h, f, d], device(s, target, b),
        )

    def attend_rows(h, query, own_token):
        scores = lax.dot_general(
            query, got[h, 1], (((1,), (1,)), ((), ())), preferred_element_type=jnp.float32
        )
        scores = jnp.where(usable, scores, MASKED_SCORE)
        peak = jnp.max(scores, axis=-1, keepdims=True)
        expo = jnp.exp2((scores - peak) * factor)
        denominator = jnp.sum(expo, axis=-1, keepdims=True)
        result = jnp.dot(expo.astype(jnp.bfloat16), got[h, 2], preferred_element_type=jnp.float32) / denominator
        return jnp.where(own_token < live, result, 0.0).astype(jnp.bfloat16)

    def attend(h, f):
        side = (s + f) % 2 * n_tensor
        row = lax.broadcasted_iota(jnp.int32, (rows, 1), 0)
        for step in range(0, n_tensor, 2):
            targets = [(t + step + i) % n_tensor for i in (1, 2)]
            spans = [spot(side + target) for target in targets]
            result = attend_rows(
                h,
                jnp.concatenate([got[h, 0, span, :] for span in spans], axis=0),
                jnp.concatenate([(side + target) * rows + row for target in targets], axis=0),
            )
            for i in range(2):
                d = step + i + 1
                if d < n_tensor:
                    done[h, spans[i], :] = result[i * rows : (i + 1) * rows]
                    att_copy(h, f, d, targets[i], t).start()
                else:
                    mixed[f, :, pl.ds(pl.multiple_of((t * heads + h) * HS, HS), HS)] = result[
                        i * rows : (i + 1) * rows
                    ]

    def back(h, f):
        def body(d, carry):
            att_copy(h, f, d, t, (t + n_tensor - d) % n_tensor).wait_recv()
            return carry

        lax.fori_loop(1, n_tensor, body, 0)

    def cut_of(p):
        return pl.ds(pl.multiple_of(p * w_cols, w_cols), w_cols)

    def part_copy(p):
        cut = cut_of(p)
        return remote(
            part_out.at[:, cut], part_in.at[:, cut], part_send.at[p], part_recv.at[p], device(1 - s, t, b)
        )

    def leave(p):
        cut = cut_of(p)
        return pltpu.make_async_copy(part_in.at[:, cut], out_ref.at[0, :, cut], out_sem.at[p])

    def project_far(k):
        p = order[k]
        for c in range(CHUNKS):
            near_copy(0, p, c, near).wait_recv()
            near_copy(1, p, c, (near + 2) % 4).wait_recv()
        cut = cut_of(p)
        part_out[:, cut] = jnp.dot(
            mixed[1], weight[:, cut], preferred_element_type=jnp.float32
        ).astype(jnp.bfloat16)
        part_copy(p).start()

    for h in range(heads):
        start_across(h)

    relay(1)
    middle = ((t == 1) | (t == 2)).astype(jnp.int32)
    inner_first = jnp.where(t == 2, 2, 1)
    inner_last = inner_first + 2 * middle
    outer_first = jnp.where(t == 1, 3, 1)
    outer_last = jnp.where(t == 2, 2, 4)
    for h in range(heads):
        start_kv_far(h, inner_first, inner_last)
    forward(order[0])
    relay(2)
    for h in range(heads):
        start_kv_far(h, outer_first, outer_last)
    forward(order[1])
    relay(3)

    for h in range(heads):
        own_arrive(h)
        arrive(h, (1, 2), 1, group)
        arrive(h, (0,), n_tensor, group)
        attend(h, 1)
        if h == 0:
            forward(order[2])
            start_own(0)
        if h == 1:
            forward(order[3])
        if h == 2:
            start_own(1)
            start_own(2)
    arrive(0, (0,), 1, n_tensor)
    attend(0, 0)
    for h in range(heads):
        back(h, 1)
    project_far(0)
    project_far(1)
    arrive(1, (0,), 1, n_tensor)
    attend(1, 0)
    project_far(2)
    project_far(3)
    arrive(2, (0,), 1, n_tensor)
    attend(2, 0)
    for h in range(heads):
        back(h, 0)
    for p in order:
        cut = cut_of(p)
        own_part[:, cut] = jnp.dot(mixed[0], weight[:, cut], preferred_element_type=jnp.float32)
    for p in order:
        cut = cut_of(p)
        part_copy(p).wait_recv()
        part_in[:, cut] = (own_part[:, cut] + part_in[:, cut].astype(jnp.float32)).astype(jnp.bfloat16)
        leave(p).start()

    for h in range(heads):
        def sent(e, carry):
            for j in range(3):
                qkv_copy(h, j, e, peer_of(e), (s, t)).wait_send()
            return carry

        lax.fori_loop(1, group, sent, 0)

        def att_sent(d, carry):
            for f in range(2):
                att_copy(h, f, d, (t + d) % n_tensor, t).wait_send()
            return carry

        lax.fori_loop(1, n_tensor, att_sent, 0)
    for c in range(CHUNKS):
        for k in range(n_tensor):
            @pl.when((t >= k) & (t < n_tensor - 1))
            def _():
                up_copy(t - k, c).wait_send()

            @pl.when((t + k < n_tensor) & (t > 0))
            def _():
                down_copy(t + k, c).wait_send()

        for p in range(n_tensor):
            far_copy(p, c, b).wait_send()
            near_copy(0, p, c, b).wait_send()
            near_copy(1, p, c, far).wait_send()

    for p in range(n_tensor):
        part_copy(p).wait_send()
        leave(p).wait()


def fused(axes, sizes, queries, keys, values, lengths, out_weight):
    n_seq, n_tensor, n_bucket = sizes
    rows, width = queries.shape[1:]
    group = n_seq * n_tensor
    heads = width // HS // group
    total = group * rows
    half = width // n_seq
    anywhere = pl.BlockSpec(memory_space=pl.ANY)
    dma = pltpu.SemaphoreType.DMA
    return pl.pallas_call(
        functools.partial(whole_kernel, axes, sizes),
        out_shape=jax.ShapeDtypeStruct(queries.shape, queries.dtype),
        in_specs=[pl.BlockSpec(memory_space=pltpu.SMEM), anywhere, anywhere, anywhere, anywhere],
        out_specs=anywhere,
        scratch_shapes=[
            pltpu.VMEM((3, rows, width), jnp.bfloat16),
            pltpu.VMEM((heads, 3, total, HS), jnp.bfloat16),
            pltpu.VMEM((heads, total, HS), jnp.bfloat16),
            pltpu.VMEM((n_seq, rows, half), jnp.bfloat16),
            pltpu.VMEM((half, width), jnp.bfloat16),
            pltpu.VMEM((rows, width), jnp.bfloat16),
            pltpu.VMEM((rows, width), jnp.bfloat16),
            pltpu.VMEM((rows, width), jnp.float32),
            dma((4,)),
            dma((heads, 3)),
            dma((heads, 3, group)),
            dma((heads, 3, group)),
            dma((heads, 2, n_tensor)),
            dma((heads, 2, n_tensor)),
            dma((n_tensor, CHUNKS)),
            dma((n_tensor, CHUNKS)),
            dma((n_tensor, CHUNKS)),
            dma((n_tensor, CHUNKS)),
            dma((n_tensor, CHUNKS)),
            dma((2, n_tensor, CHUNKS)),
            dma((2, n_tensor, CHUNKS)),
            dma((n_tensor,)),
            dma((n_tensor,)),
            dma((n_tensor,)),
        ],
        compiler_params=pltpu.CompilerParams(
            collective_id=0, has_side_effects=True, vmem_limit_bytes=56 * 1024 * 1024,
        ),
    )(lengths, queries, keys, values, out_weight)


def solution(mesh):
    in_specs = (
        P("bucket", ("seq", "tensor"), None),
        P("bucket", ("seq", "tensor"), None),
        P("bucket", ("seq", "tensor"), None),
        P("bucket"),
        P(("seq", "bucket"), "tensor"),
    )
    out_specs = P("bucket", ("seq", "tensor"), None)
    sizes = tuple(mesh.shape[name] for name in ("seq", "tensor", "bucket"))

    def step(queries, keys, values, lengths, out_weight):
        head_count = queries.shape[2] // HS
        fits = sizes[0] == 2 and sizes[1] == sizes[2] == 4 and head_count % (sizes[0] * sizes[1]) == 0
        if fits:
            return fused(mesh.axis_names, sizes, queries, keys, values, lengths, out_weight)
        return shards(queries, keys, values, lengths, out_weight)

    return jax.shard_map(step, mesh=mesh, in_specs=in_specs, out_specs=out_specs, check_vma=False)
```

time: 132 us -> 111 us (0.84)
  Pallas kernels: 128 us -> 108 us
    pallas_call x1, Pallas kernels: 128 us -> 108 us  [fused(): pl.pallas_call(functools.partial(whole_kernel, axes, sizes), out_shape=ja...]
where the time goes in v1:
time: 111 us
  Pallas kernels  108 us (97%)
  local copies, waits for them, and re-layouts  2.06 us (2%)
    pallas_call x1, Pallas kernels, fused(): pl.pallas_call(functools.partial(whole_kernel, axes, sizes), out_shape=ja...  108 us

profile of v1, /device:TPU:0, one launch (start us, length us, event | category | flops | bytes accessed | tf_op | source)
XLA Modules:
  0.0 110.7 jit_solution(16504960338928194450)
XLA Ops:
  0.7 107.9 %shard_map.55 = bf16[1,128,3072]{2,1,0:T(8,128)(2,1)} custom-call(s32[1]{0:T(128)S(6)} %copy.7.len_ref, bf16[1,128,3072]{2,1,0:T(8,128)(2,1)} %q_ref.1, bf16[1,128,3072]{2,1,0:T(8,128)(2,1)} %k_ref.1, bf16[1,128,3072]{2,1,0:T(8,128)(2,1)} %v_ref.1, bf16[384,768]{1,0:T(8,128)(2,1)} %w_ref.1), custom_call_target="tpu_custom_call" | custom-call | tf_op jit(solution)/shard_map/pallas_call | solution.py:449
  108.6 2.1 %copy.8 = bf16[1,128,3072]{2,1,0:T(8,128)(2,1)} copy(bf16[1,128,3072]{2,1,0:T(8,128)(2,1)} %shard_map.55) | data formatting | bytes 1572864

commit v2 on v1

--- a/solution.py
+++ b/solution.py
@@ -12,9 +12,6 @@
 
 
 MASKED_SCORE = -1e30
-
-
-CHUNKS = 2
 
 
 def shards(queries, keys, values, lengths, out_weight):
@@ -89,7 +86,7 @@
     axes, sizes, len_ref, q_ref, k_ref, v_ref, w_ref, out_ref,
     held, got, done, mixed, weight, part_out, part_in, own_part, load_sem, own_sem,
     qkv_send, qkv_recv, att_send, att_recv, up_send, down_send, line_recv,
-    far_send, far_recv, near_send, near_recv, part_send, part_recv, out_sem,
+    far_send, far_recv, near_send, near_recv, part_send, part_recv,
 ):
     n_seq, n_tensor, n_bucket = sizes
     s, t, b = lax.axis_index("seq"), lax.axis_index("tensor"), lax.axis_index("bucket")
@@ -164,11 +161,10 @@
     def start_own(h):
         start_stream(h, (0,), 1, n_tensor)
 
-    chunk = w_rows // CHUNKS
-
     def piece(row_block, col_block, c):
         return weight.at[
-            pl.ds(pl.multiple_of(row_block * w_rows + c * chunk, chunk), chunk),
+            c,
+            pl.ds(pl.multiple_of(row_block * HS, HS), HS),
             pl.ds(pl.multiple_of(col_block * w_cols, w_cols), w_cols),
         ]
 
@@ -221,15 +217,14 @@
             spread(t + k, c)
 
     def relay(k):
-        for c in range(CHUNKS):
+        for c in range(heads):
             relay_chunk(k, c)
 
-    own_piece = weight.at[
-        pl.ds(pl.multiple_of(b * w_rows, w_rows), w_rows),
-        pl.ds(pl.multiple_of(t * w_cols, w_cols), w_cols),
-    ]
-    weight_load = pltpu.make_async_copy(w_ref, own_piece, load_sem.at[3])
-    weight_load.start()
+    def weight_load(c):
+        return pltpu.make_async_copy(w_ref.at[pl.ds(c * HS, HS), :], piece(b, t, c), load_sem.at[3 + c])
+
+    for c in range(heads):
+        weight_load(c).start()
 
     def load(j):
         return pltpu.make_async_copy(streams[j].at[0], held.at[j], load_sem.at[j])
@@ -252,9 +247,9 @@
         for j in range(3):
             own_copy(h, j).start()
     pl.semaphore_wait(barrier, group + 1)
-    weight_load.wait()
-
-    for c in range(CHUNKS):
+    for c in range(heads):
+        weight_load(c).wait()
+
         @pl.when(t < n_tensor - 1)
         def _():
             up_copy(t, c).start()
@@ -271,7 +266,7 @@
     order = (t, 1 - t + 4 * upper, 2 - upper, 3 - 3 * upper)
 
     def forward(p):
-        for c in range(CHUNKS):
+        for c in range(heads):
             far_copy(p, c, far).wait_recv()
             near_copy(1, p, c, far).start()
 
@@ -280,9 +275,9 @@
     factor = HS ** (-0.5) * math.log2(math.e)
 
     def att_copy(h, f, d, target, source):
-        cols = pl.ds(pl.multiple_of((source * heads + h) * HS, HS), HS)
-        return remote(
-            done.at[h, spot((s + f) % 2 * n_tensor + target), :], mixed.at[f, :, cols],
+        cols = pl.ds(pl.multiple_of(source * HS, HS), HS)
+        return remote(
+            done.at[h, spot((s + f) % 2 * n_tensor + target), :], mixed.at[f, h, :, cols],
             att_send.at[h, f, d], att_recv.at[h, f, d], device(s, target, b),
         )
 
@@ -314,7 +309,7 @@
                     done[h, spans[i], :] = result[i * rows : (i + 1) * rows]
                     att_copy(h, f, d, targets[i], t).start()
                 else:
-                    mixed[f, :, pl.ds(pl.multiple_of((t * heads + h) * HS, HS), HS)] = result[
+                    mixed[f, h, :, pl.ds(pl.multiple_of(t * HS, HS), HS)] = result[
                         i * rows : (i + 1) * rows
                     ]
 
@@ -334,19 +329,26 @@
             part_out.at[:, cut], part_in.at[:, cut], part_send.at[p], part_recv.at[p], device(1 - s, t, b)
         )
 
-    def leave(p):
+    def product(f, h, cut):
+        return jnp.dot(mixed[f, h], weight[h, :, cut], preferred_element_type=jnp.float32)
+
+    def own_product(h):
+        for p in order:
+            cut = cut_of(p)
+            own_part[:, cut] = product(0, h, cut) if h == 0 else own_part[:, cut] + product(0, h, cut)
+
+    def finish(p):
         cut = cut_of(p)
-        return pltpu.make_async_copy(part_in.at[:, cut], out_ref.at[0, :, cut], out_sem.at[p])
+        part_copy(p).wait_recv()
+        out_ref[0, :, cut] = (own_part[:, cut] + part_in[:, cut].astype(jnp.float32)).astype(jnp.bfloat16)
 
     def project_far(k):
         p = order[k]
-        for c in range(CHUNKS):
+        for c in range(heads):
             near_copy(0, p, c, near).wait_recv()
             near_copy(1, p, c, (near + 2) % 4).wait_recv()
         cut = cut_of(p)
-        part_out[:, cut] = jnp.dot(
-            mixed[1], weight[:, cut], preferred_element_type=jnp.float32
-        ).astype(jnp.bfloat16)
+        part_out[:, cut] = sum(product(1, h, cut) for h in range(heads)).astype(jnp.bfloat16)
         part_copy(p).start()
 
     for h in range(heads):
@@ -374,34 +376,28 @@
         attend(h, 1)
         if h == 0:
             forward(order[2])
-            start_own(0)
         if h == 1:
             forward(order[3])
-        if h == 2:
-            start_own(1)
-            start_own(2)
+            start_own(0)
+    for h in range(heads):
+        back(h, 1)
+    start_own(1)
+    start_own(2)
+    project_far(0)
     arrive(0, (0,), 1, n_tensor)
     attend(0, 0)
-    for h in range(heads):
-        back(h, 1)
-    project_far(0)
     project_far(1)
     arrive(1, (0,), 1, n_tensor)
     attend(1, 0)
     project_far(2)
-    project_far(3)
     arrive(2, (0,), 1, n_tensor)
     attend(2, 0)
+    project_far(3)
     for h in range(heads):
         back(h, 0)
+        own_product(h)
     for p in order:
-        cut = cut_of(p)
-        own_part[:, cut] = jnp.dot(mixed[0], weight[:, cut], preferred_element_type=jnp.float32)
-    for p in order:
-        cut = cut_of(p)
-        part_copy(p).wait_recv()
-        part_in[:, cut] = (own_part[:, cut] + part_in[:, cut].astype(jnp.float32)).astype(jnp.bfloat16)
-        leave(p).start()
+        finish(p)
 
     for h in range(heads):
         def sent(e, carry):
@@ -417,7 +413,7 @@
             return carry
 
         lax.fori_loop(1, n_tensor, att_sent, 0)
-    for c in range(CHUNKS):
+    for c in range(heads):
         for k in range(n_tensor):
             @pl.when((t >= k) & (t < n_tensor - 1))
             def _():
@@ -434,7 +430,6 @@
 
     for p in range(n_tensor):
         part_copy(p).wait_send()
-        leave(p).wait()
 
 
 def fused(axes, sizes, queries, keys, values, lengths, out_weight):
@@ -443,44 +438,42 @@
     group = n_seq * n_tensor
     heads = width // HS // group
     total = group * rows
-    half = width // n_seq
     anywhere = pl.BlockSpec(memory_space=pl.ANY)
     dma = pltpu.SemaphoreType.DMA
     return pl.pallas_call(
         functools.partial(whole_kernel, axes, sizes),
         out_shape=jax.ShapeDtypeStruct(queries.shape, queries.dtype),
         in_specs=[pl.BlockSpec(memory_space=pltpu.SMEM), anywhere, anywhere, anywhere, anywhere],
-        out_specs=anywhere,
+        out_specs=pl.BlockSpec(memory_space=pltpu.VMEM),
         scratch_shapes=[
             pltpu.VMEM((3, rows, width), jnp.bfloat16),
             pltpu.VMEM((heads, 3, total, HS), jnp.bfloat16),
             pltpu.VMEM((heads, total, HS), jnp.bfloat16),
-            pltpu.VMEM((n_seq, rows, half), jnp.bfloat16),
-            pltpu.VMEM((half, width), jnp.bfloat16),
+            pltpu.VMEM((n_seq, heads, rows, n_tensor * HS), jnp.bfloat16),
+            pltpu.VMEM((heads, n_bucket * HS, width), jnp.bfloat16),
             pltpu.VMEM((rows, width), jnp.bfloat16),
             pltpu.VMEM((rows, width), jnp.bfloat16),
             pltpu.VMEM((rows, width), jnp.float32),
-            dma((4,)),
+            dma((3 + heads,)),
             dma((heads, 3)),
             dma((heads, 3, group)),
             dma((heads, 3, group)),
             dma((heads, 2, n_tensor)),
             dma((heads, 2, n_tensor)),
-            dma((n_tensor, CHUNKS)),
-            dma((n_tensor, CHUNKS)),
-            dma((n_tensor, CHUNKS)),
-            dma((n_tensor, CHUNKS)),
-            dma((n_tensor, CHUNKS)),
-            dma((2, n_tensor, CHUNKS)),
-            dma((2, n_tensor, CHUNKS)),
-            dma((n_tensor,)),
+            dma((n_tensor, heads)),
+            dma((n_tensor, heads)),
+            dma((n_tensor, heads)),
+            dma((n_tensor, heads)),
+            dma((n_tensor, heads)),
+            dma((2, n_tensor, heads)),
+            dma((2, n_tensor, heads)),
             dma((n_tensor,)),
             dma((n_tensor,)),
         ],
         compiler_params=pltpu.CompilerParams(
-            collective_id=0, has_side_effects=True, vmem_limit_bytes=56 * 1024 * 1024,
+            collective_id=0, has_side_effects=True, vmem_limit_bytes=32 * 1024 * 1024,
         ),
-    )(lengths, queries, keys, values, out_weight)
+    )(lengths, *(pltpu.with_memory_space_constraint(x, pltpu.HBM) for x in (queries, keys, values, out_weight)))
 
 
 def solution(mesh):

time: 111 us -> 107 us (0.964)
  Pallas kernels: 108 us -> 105 us
  local copies, waits for them, and re-layouts: 2.06 us -> 0.88 us
    pallas_call x1, Pallas kernels: 108 us -> 105 us  [fused(): pl.pallas_call(functools.partial(whole_kernel, axes, sizes), out_shape=ja...]
    unnamed x1, local copies, waits for them, and re-layouts: 2.06 us -> 0.88 us
where the time goes in v2:
time: 107 us
  Pallas kernels  105 us (98%)
    pallas_call x1, Pallas kernels, fused(): pl.pallas_call(functools.partial(whole_kernel, axes, sizes), out_shape=ja...  105 us

profile of v2, /device:TPU:0, one launch (start us, length us, event | category | flops | bytes accessed | tf_op | source)
XLA Modules:
  0.0 106.9 jit_solution(11951100703665474339)
XLA Ops:
  0.7 105.4 %shard_map.55 = bf16[1,128,3072]{2,1,0:T(8,128)(2,1)S(1)} custom-call(s32[1]{0:T(128)S(6)} %copy.7.len_ref, bf16[1,128,3072]{2,1,0:T(8,128)(2,1)} %q_ref.1, bf16[1,128,3072]{2,1,0:T(8,128)(2,1)} %k_ref.1, bf16[1,128,3072]{2,1,0:T(8,128)(2,1)} %v_ref.1, bf16[384,768]{1,0:T(8,128)(2,1)} %w_ref.1), custom_call_target="tpu_custom_call" | custom-call | tf_op jit(solution)/shard_map/pallas_call | solution.py:443
  106.0 0.9 copy.8

commit v3 on v2

--- a/solution.py
+++ b/solution.py
@@ -84,7 +84,7 @@
 
 def whole_kernel(
     axes, sizes, len_ref, q_ref, k_ref, v_ref, w_ref, out_ref,
-    held, got, done, mixed, weight, part_out, part_in, own_part, load_sem, own_sem,
+    held, got, done, mixed, weight, part_out, part_in, own_part, load_sem, ready,
     qkv_send, qkv_recv, att_send, att_recv, up_send, down_send, line_recv,
     far_send, far_recv, near_send, near_recv, part_send, part_recv,
 ):
@@ -95,7 +95,6 @@
     width = q_ref.shape[2]
     heads = width // HS // group
     w_rows, w_cols = w_ref.shape
-    live = len_ref[0]
 
     def device(ds, dt, db):
         place = {"seq": ds, "tensor": dt, "bucket": db}
@@ -120,46 +119,45 @@
     def source_of(e):
         return (s + e // n_tensor) % 2, (t + n_tensor - e % n_tensor) % n_tensor
 
-    def qkv_copy(h, j, e, to, source):
+    def drain(ref, sem):
+        pltpu.make_async_copy(ref, ref, sem).wait()
+
+    def qkv_copy(h, j, to, f):
         cols = pl.ds(pl.multiple_of(((to[0] * n_tensor + to[1]) * heads + h) * HS, HS), HS)
         return remote(
             held.at[j, :, cols],
-            got.at[h, j, spot(source[0] * n_tensor + source[1]), :],
-            qkv_send.at[h, j, e],
-            qkv_recv.at[h, j, e],
+            got.at[h, j, spot(me), :],
+            qkv_send,
+            qkv_recv.at[h, f if j == 0 else 2],
             device(to[0], to[1], b),
         )
 
-    def start_stream(h, js, first, last):
-        def body(e, carry):
+    def start_stream(h, js, first, last, f):
+        def body(d, carry):
             for j in js:
-                qkv_copy(h, j, e, peer_of(e), (s, t)).start()
+                qkv_copy(h, j, peer_of(f * n_tensor + d), f).start()
             return carry
 
         lax.fori_loop(first, last, body, 0)
 
-    def arrive(h, js, first, last):
-        def body(e, carry):
-            for j in js:
-                qkv_copy(h, j, e, (s, t), source_of(e)).wait_recv()
-            return carry
-
-        lax.fori_loop(first, last, body, 0)
-
-    def own_arrive(h):
-        for j in range(3):
-            own_copy(h, j).wait()
+    def side_rows(f):
+        return pl.ds(pl.multiple_of((s + f) % 2 * n_tensor * rows, rows), n_tensor * rows)
+
+    def arrive_kv(h):
+        drain(got.at[h, pl.ds(1, 2)], qkv_recv.at[h, 2])
+
+    def arrive_q(h, f):
+        drain(got.at[h, 0, side_rows(f), :], qkv_recv.at[h, f])
 
     def start_across(h):
-        start_stream(h, (1, 2, 0), n_tensor, n_tensor + 1)
+        start_stream(h, (1, 2, 0), 0, 1, 1)
 
     def start_kv_far(h, first=1, last=4):
-        start_stream(h, (1, 2), first, last)
-        start_stream(h, (1, 2, 0), n_tensor + first, n_tensor + last)
-
+        start_stream(h, (1, 2), first, last, 0)
+        start_stream(h, (1, 2, 0), first, last, 1)
 
     def start_own(h):
-        start_stream(h, (0,), 1, n_tensor)
+        start_stream(h, (0,), 1, n_tensor, 0)
 
     def piece(row_block, col_block, c):
         return weight.at[
@@ -168,32 +166,34 @@
             pl.ds(pl.multiple_of(col_block * w_cols, w_cols), w_cols),
         ]
 
+    def cut_of(p):
+        return pl.ds(pl.multiple_of(p * w_cols, w_cols), w_cols)
+
     far, near = (b + 2) % 4, b + 1 - 2 * (b % 2)
 
     def up_copy(p, c):
         return remote(
-            piece(b, p, c), piece(b, p, c), up_send.at[p, c], line_recv.at[p, c], device(s, t + 1, b)
+            piece(b, p, c), piece(b, p, c), up_send, line_recv.at[p, c], device(s, t + 1, b)
         )
 
     def down_copy(p, c):
         return remote(
-            piece(b, p, c), piece(b, p, c), down_send.at[p, c], line_recv.at[p, c], device(s, t - 1, b)
+            piece(b, p, c), piece(b, p, c), down_send, line_recv.at[p, c], device(s, t - 1, b)
         )
 
     def far_copy(p, c, row_block):
         return remote(
-            piece(row_block, p, c), piece(row_block, p, c), far_send.at[p, c], far_recv.at[p, c], device(s, t, far)
-        )
-
-    def near_copy(k, p, c, row_block):
-        return remote(
-            piece(row_block, p, c), piece(row_block, p, c),
-            near_send.at[k, p, c], near_recv.at[k, p, c], device(s, t, near),
+            piece(row_block, p, c), piece(row_block, p, c), far_send, far_recv.at[p], device(s, t, far)
+        )
+
+    def near_copy(p, c, row_block):
+        return remote(
+            piece(row_block, p, c), piece(row_block, p, c), near_send, near_recv.at[p], device(s, t, near)
         )
 
     def spread(p, c):
         far_copy(p, c, b).start()
-        near_copy(0, p, c, b).start()
+        near_copy(p, c, b).start()
 
     def relay_chunk(k, c):
         @pl.when(t >= k)
@@ -221,35 +221,47 @@
             relay_chunk(k, c)
 
     def weight_load(c):
-        return pltpu.make_async_copy(w_ref.at[pl.ds(c * HS, HS), :], piece(b, t, c), load_sem.at[3 + c])
+        return pltpu.make_async_copy(w_ref.at[pl.ds(c * HS, HS), :], piece(b, t, c), load_sem.at[1])
 
     for c in range(heads):
         weight_load(c).start()
 
     def load(j):
-        return pltpu.make_async_copy(streams[j].at[0], held.at[j], load_sem.at[j])
+        return pltpu.make_async_copy(streams[j].at[0], held.at[j], load_sem.at[0])
 
     def own_copy(h, j):
         cols = pl.ds(pl.multiple_of((me * heads + h) * HS, HS), HS)
-        return pltpu.make_async_copy(streams[j].at[0, :, cols], got.at[h, j, spot(me), :], own_sem.at[h, j])
-
-    def greet(where):
-        pl.semaphore_signal(barrier, inc=1, device_id=where, device_id_type=pl.DeviceIdType.MESH)
-
-    for e in range(1, group):
-        to = peer_of(e)
-        greet(device(to[0], to[1], b))
-    greet(device(s, t, far))
-    greet(device(s, t, near))
+        return pltpu.make_async_copy(
+            streams[j].at[0, :, cols], got.at[h, j, spot(me), :], qkv_recv.at[h, 0 if j == 0 else 2]
+        )
+
+    def greet(semaphore, where):
+        pl.semaphore_signal(semaphore, inc=1, device_id=where, device_id_type=pl.DeviceIdType.MESH)
+
+    def greet_group(semaphore):
+        greet(semaphore, device(1 - s, t, b))
+
+        @pl.when(t > 0)
+        def _():
+            greet(semaphore, device(s, t - 1, b))
+
+        @pl.when(t < n_tensor - 1)
+        def _():
+            greet(semaphore, device(s, t + 1, b))
+
+    beside = 1 + (t > 0).astype(jnp.int32) + (t < n_tensor - 1).astype(jnp.int32)
+    greet(barrier, device(s, t, far))
+    greet(barrier, device(s, t, near))
+    greet_group(barrier)
     for j in (1, 2, 0):
         load(j).start()
     for h in range(heads):
         for j in range(3):
             own_copy(h, j).start()
-    pl.semaphore_wait(barrier, group + 1)
+    pl.semaphore_wait(barrier, beside + 2)
+    drain(weight.at[:, pl.ds(pl.multiple_of(b * HS, HS), HS), cut_of(t)], load_sem.at[1])
+
     for c in range(heads):
-        weight_load(c).wait()
-
         @pl.when(t < n_tensor - 1)
         def _():
             up_copy(t, c).start()
@@ -259,26 +271,29 @@
             down_copy(t, c).start()
 
         spread(t, c)
-    for j in (1, 2, 0):
-        load(j).wait()
+    for k in range(3):
+        greet_group(ready.at[k])
+        pl.semaphore_wait(ready.at[k], beside)
+    drain(held, load_sem.at[0])
+    live = len_ref[0]
 
     upper = t // 2
     order = (t, 1 - t + 4 * upper, 2 - upper, 3 - 3 * upper)
 
     def forward(p):
+        drain(weight.at[:, pl.ds(pl.multiple_of(far * HS, HS), HS), cut_of(p)], far_recv.at[p])
         for c in range(heads):
-            far_copy(p, c, far).wait_recv()
-            near_copy(1, p, c, far).start()
+            near_copy(p, c, far).start()
 
     total = group * rows
     usable = lax.broadcasted_iota(jnp.int32, (1, total), 1) < live
     factor = HS ** (-0.5) * math.log2(math.e)
 
-    def att_copy(h, f, d, target, source):
+    def att_copy(h, f, target, source):
         cols = pl.ds(pl.multiple_of(source * HS, HS), HS)
         return remote(
             done.at[h, spot((s + f) % 2 * n_tensor + target), :], mixed.at[f, h, :, cols],
-            att_send.at[h, f, d], att_recv.at[h, f, d], device(s, target, b),
+            att_send, att_recv.at[heads if f else h], device(s, target, b),
         )
 
     def attend_rows(h, query, own_token):
@@ -307,26 +322,35 @@
                 d = step + i + 1
                 if d < n_tensor:
                     done[h, spans[i], :] = result[i * rows : (i + 1) * rows]
-                    att_copy(h, f, d, targets[i], t).start()
+                    att_copy(h, f, targets[i], t).start()
                 else:
                     mixed[f, h, :, pl.ds(pl.multiple_of(t * HS, HS), HS)] = result[
                         i * rows : (i + 1) * rows
                     ]
 
-    def back(h, f):
-        def body(d, carry):
-            att_copy(h, f, d, t, (t + n_tensor - d) % n_tensor).wait_recv()
-            return carry
-
-        lax.fori_loop(1, n_tensor, body, 0)
-
-    def cut_of(p):
-        return pl.ds(pl.multiple_of(p * w_cols, w_cols), w_cols)
+    def back_far():
+        drain(mixed.at[1, :, :, pl.ds(0, (n_tensor - 1) * HS)], att_recv.at[heads])
+
+    def back_own(h):
+        drain(mixed.at[0, h, :, pl.ds(0, (n_tensor - 1) * HS)], att_recv.at[h])
+
+    def weight_sent():
+        for n in range(1, n_tensor):
+            @pl.when(t == n - 1)
+            def _():
+                drain(weight.at[:, pl.ds(0, HS), pl.ds(0, n * w_cols)], up_send)
+
+            @pl.when(t == n_tensor - n)
+            def _():
+                drain(weight.at[:, pl.ds(0, HS), pl.ds(0, n * w_cols)], down_send)
+
+        drain(weight.at[:, pl.ds(0, HS), :], far_send)
+        drain(weight.at[:, pl.ds(0, 2 * HS), :], near_send)
 
     def part_copy(p):
         cut = cut_of(p)
         return remote(
-            part_out.at[:, cut], part_in.at[:, cut], part_send.at[p], part_recv.at[p], device(1 - s, t, b)
+            part_out.at[:, cut], part_in.at[:, cut], part_send, part_recv.at[p], device(1 - s, t, b)
         )
 
     def product(f, h, cut):
@@ -339,17 +363,17 @@
 
     def finish(p):
         cut = cut_of(p)
+        mine = own_part[:, cut] + product(0, heads - 1, cut)
         part_copy(p).wait_recv()
-        out_ref[0, :, cut] = (own_part[:, cut] + part_in[:, cut].astype(jnp.float32)).astype(jnp.bfloat16)
+        out_ref[0, :, cut] = (mine + part_in[:, cut].astype(jnp.float32)).astype(jnp.bfloat16)
 
     def project_far(k):
         p = order[k]
-        for c in range(heads):
-            near_copy(0, p, c, near).wait_recv()
-            near_copy(1, p, c, (near + 2) % 4).wait_recv()
         cut = cut_of(p)
+        drain(weight.at[:, pl.ds(0, 2 * HS), cut], near_recv.at[p])
         part_out[:, cut] = sum(product(1, h, cut) for h in range(heads)).astype(jnp.bfloat16)
         part_copy(p).start()
+
 
     for h in range(heads):
         start_across(h)
@@ -370,66 +394,38 @@
     relay(3)
 
     for h in range(heads):
-        own_arrive(h)
-        arrive(h, (1, 2), 1, group)
-        arrive(h, (0,), n_tensor, group)
+        arrive_kv(h)
+        arrive_q(h, 1)
         attend(h, 1)
         if h == 0:
             forward(order[2])
         if h == 1:
             forward(order[3])
             start_own(0)
-    for h in range(heads):
-        back(h, 1)
+    back_far()
     start_own(1)
     start_own(2)
     project_far(0)
-    arrive(0, (0,), 1, n_tensor)
+    arrive_q(0, 0)
     attend(0, 0)
     project_far(1)
-    arrive(1, (0,), 1, n_tensor)
+    arrive_q(1, 0)
     attend(1, 0)
     project_far(2)
-    arrive(2, (0,), 1, n_tensor)
+    arrive_q(2, 0)
     attend(2, 0)
     project_far(3)
-    for h in range(heads):
-        back(h, 0)
-        own_product(h)
+    weight_sent()
+    back_own(0)
+    own_product(0)
+    back_own(1)
+    own_product(1)
+    back_own(2)
     for p in order:
         finish(p)
-
-    for h in range(heads):
-        def sent(e, carry):
-            for j in range(3):
-                qkv_copy(h, j, e, peer_of(e), (s, t)).wait_send()
-            return carry
-
-        lax.fori_loop(1, group, sent, 0)
-
-        def att_sent(d, carry):
-            for f in range(2):
-                att_copy(h, f, d, (t + d) % n_tensor, t).wait_send()
-            return carry
-
-        lax.fori_loop(1, n_tensor, att_sent, 0)
-    for c in range(heads):
-        for k in range(n_tensor):
-            @pl.when((t >= k) & (t < n_tensor - 1))
-            def _():
-                up_copy(t - k, c).wait_send()
-
-            @pl.when((t + k < n_tensor) & (t > 0))
-            def _():
-                down_copy(t + k, c).wait_send()
-
-        for p in range(n_tensor):
-            far_copy(p, c, b).wait_send()
-            near_copy(0, p, c, b).wait_send()
-            near_copy(1, p, c, far).wait_send()
-
-    for p in range(n_tensor):
-        part_copy(p).wait_send()
+    drain(got.at[:, :, pl.ds(0, (group - 1) * rows), :], qkv_send)
+    drain(done.at[:, pl.ds(0, n_seq * (n_tensor - 1) * rows), :], att_send)
+    drain(part_out, part_send)
 
 
 def fused(axes, sizes, queries, keys, values, lengths, out_weight):
@@ -454,20 +450,20 @@
             pltpu.VMEM((rows, width), jnp.bfloat16),
             pltpu.VMEM((rows, width), jnp.bfloat16),
             pltpu.VMEM((rows, width), jnp.float32),
-            dma((3 + heads,)),
+            dma((2,)),
+            pltpu.SemaphoreType.REGULAR((3,)),
+            dma,
             dma((heads, 3)),
-            dma((heads, 3, group)),
-            dma((heads, 3, group)),
-            dma((heads, 2, n_tensor)),
-            dma((heads, 2, n_tensor)),
+            dma,
+            dma((heads + 1,)),
+            dma,
+            dma,
             dma((n_tensor, heads)),
-            dma((n_tensor, heads)),
-            dma((n_tensor, heads)),
-            dma((n_tensor, heads)),
-            dma((n_tensor, heads)),
-            dma((2, n_tensor, heads)),
-            dma((2, n_tensor, heads)),
+            dma,
             dma((n_tensor,)),
+            dma,
+            dma((n_tensor,)),
+            dma,
             dma((n_tensor,)),
         ],
         compiler_params=pltpu.CompilerParams(

time: 107 us -> 104 us (0.972)
  Pallas kernels: 105 us -> 103 us
    pallas_call x1, Pallas kernels: 105 us -> 103 us  [fused(): pl.pallas_call(functools.partial(whole_kernel, axes, sizes), out_shape=ja...]
where the time goes in v3:
time: 104 us
  Pallas kernels  103 us (99%)
    pallas_call x1, Pallas kernels, fused(): pl.pallas_call(functools.partial(whole_kernel, axes, sizes), out_shape=ja...  103 us

profile of v3, /device:TPU:0, one launch (start us, length us, event | category | flops | bytes accessed | tf_op | source)
XLA Modules:
  0.0 104.2 jit_solution(9466762784547724990)
XLA Ops:
  0.7 102.7 %shard_map.55 = bf16[1,128,3072]{2,1,0:T(8,128)(2,1)S(1)} custom-call(s32[1]{0:T(128)S(6)} %copy.7.len_ref, bf16[1,128,3072]{2,1,0:T(8,128)(2,1)} %q_ref.1, bf16[1,128,3072]{2,1,0:T(8,128)(2,1)} %k_ref.1, bf16[1,128,3072]{2,1,0:T(8,128)(2,1)} %v_ref.1, bf16[384,768]{1,0:T(8,128)(2,1)} %w_ref.1), custom_call_target="tpu_custom_call" | custom-call | tf_op jit(solution)/shard_map/pallas_call | solution.py:439
  103.3 0.9 copy.8

commit v4 on v3

--- a/solution.py
+++ b/solution.py
@@ -113,51 +113,54 @@
     def spot(place):
         return pl.ds(pl.multiple_of(place * rows, rows), rows)
 
-    def peer_of(e):
-        return (s + e // n_tensor) % 2, (t + e % n_tensor) % n_tensor
-
-    def source_of(e):
-        return (s + e // n_tensor) % 2, (t + n_tensor - e % n_tensor) % n_tensor
+    toward = 1 - 2 * (t // (n_tensor // 2))
+
+    def along(i):
+        return (t + toward * i + 2 * n_tensor) % n_tensor
 
     def drain(ref, sem):
         pltpu.make_async_copy(ref, ref, sem).wait()
 
-    def qkv_copy(h, j, to, f):
-        cols = pl.ds(pl.multiple_of(((to[0] * n_tensor + to[1]) * heads + h) * HS, HS), HS)
-        return remote(
-            held.at[j, :, cols],
-            got.at[h, j, spot(me), :],
+    part_rows = rows // 2
+    bands = ((0, 0, rows), (1, 0, part_rows), (1, part_rows, part_rows))
+
+    def band_rows(g, place):
+        f, first, count = bands[g]
+        return pl.ds(pl.multiple_of(place * rows + first, part_rows), count)
+
+    def send_copy(h, j, i, f, g):
+        dt = along(i)
+        ds = (s + f) % 2
+        cols = pl.ds(pl.multiple_of(((ds * n_tensor + dt) * heads + h) * HS, HS), HS)
+        first, count = (0, rows) if j else bands[g][1:]
+        return remote(
+            held.at[j, pl.ds(first, count), cols],
+            got.at[h, j, pl.ds(pl.multiple_of(me * rows + first, part_rows), count), :],
             qkv_send,
-            qkv_recv.at[h, f if j == 0 else 2],
-            device(to[0], to[1], b),
-        )
-
-    def start_stream(h, js, first, last, f):
-        def body(d, carry):
-            for j in js:
-                qkv_copy(h, j, peer_of(f * n_tensor + d), f).start()
+            qkv_recv.at[h, 3 if j else g],
+            device(ds, dt, b),
+        )
+
+    def start_kv(h, f, first, last):
+        def body(i, carry):
+            for j in (1, 2):
+                send_copy(h, j, i, f, 0).start()
             return carry
 
         lax.fori_loop(first, last, body, 0)
 
-    def side_rows(f):
-        return pl.ds(pl.multiple_of((s + f) % 2 * n_tensor * rows, rows), n_tensor * rows)
+    def start_q(h, g, first, last):
+        def body(i, carry):
+            send_copy(h, 0, i, bands[g][0], g).start()
+            return carry
+
+        lax.fori_loop(first, last, body, 0)
 
     def arrive_kv(h):
-        drain(got.at[h, pl.ds(1, 2)], qkv_recv.at[h, 2])
-
-    def arrive_q(h, f):
-        drain(got.at[h, 0, side_rows(f), :], qkv_recv.at[h, f])
-
-    def start_across(h):
-        start_stream(h, (1, 2, 0), 0, 1, 1)
-
-    def start_kv_far(h, first=1, last=4):
-        start_stream(h, (1, 2), first, last, 0)
-        start_stream(h, (1, 2, 0), first, last, 1)
-
-    def start_own(h):
-        start_stream(h, (0,), 1, n_tensor, 0)
+        drain(got.at[h, pl.ds(1, 2)], qkv_recv.at[h, 3])
+
+    def arrive_q(h, g):
+        drain(got.at[h, 0, pl.ds(0, n_tensor * bands[g][2]), :], qkv_recv.at[h, g])
 
     def piece(row_block, col_block, c):
         return weight.at[
@@ -232,7 +235,7 @@
     def own_copy(h, j):
         cols = pl.ds(pl.multiple_of((me * heads + h) * HS, HS), HS)
         return pltpu.make_async_copy(
-            streams[j].at[0, :, cols], got.at[h, j, spot(me), :], qkv_recv.at[h, 0 if j == 0 else 2]
+            streams[j].at[0, :, cols], got.at[h, j, spot(me), :], qkv_recv.at[h, 3 if j else 0]
         )
 
     def greet(semaphore, where):
@@ -289,11 +292,12 @@
     usable = lax.broadcasted_iota(jnp.int32, (1, total), 1) < live
     factor = HS ** (-0.5) * math.log2(math.e)
 
-    def att_copy(h, f, target, source):
-        cols = pl.ds(pl.multiple_of(source * HS, HS), HS)
-        return remote(
-            done.at[h, spot((s + f) % 2 * n_tensor + target), :], mixed.at[f, h, :, cols],
-            att_send, att_recv.at[heads if f else h], device(s, target, b),
+    def att_copy(h, g, target):
+        f, first, count = bands[g]
+        return remote(
+            done.at[h, band_rows(g, (s + f) % 2 * n_tensor + target), :],
+            mixed.at[f, h, pl.ds(first, count), pl.ds(pl.multiple_of(t * HS, HS), HS)],
+            att_send, att_recv.at[heads + g - 1 if f else h], device(s, target, b),
         )
 
     def attend_rows(h, query, own_token):
@@ -307,29 +311,29 @@
         result = jnp.dot(expo.astype(jnp.bfloat16), got[h, 2], preferred_element_type=jnp.float32) / denominator
         return jnp.where(own_token < live, result, 0.0).astype(jnp.bfloat16)
 
-    def attend(h, f):
+    def attend(h, g):
+        f, first, count = bands[g]
         side = (s + f) % 2 * n_tensor
-        row = lax.broadcasted_iota(jnp.int32, (rows, 1), 0)
-        for step in range(0, n_tensor, 2):
-            targets = [(t + step + i) % n_tensor for i in (1, 2)]
-            spans = [spot(side + target) for target in targets]
+        row = first + lax.broadcasted_iota(jnp.int32, (count, 1), 0)
+        together = 2 * rows // count
+        for step in range(0, n_tensor, together):
+            targets = [along(step + i + 1) for i in range(together)]
+            spans = [band_rows(g, side + target) for target in targets]
             result = attend_rows(
                 h,
                 jnp.concatenate([got[h, 0, span, :] for span in spans], axis=0),
                 jnp.concatenate([(side + target) * rows + row for target in targets], axis=0),
             )
-            for i in range(2):
-                d = step + i + 1
-                if d < n_tensor:
-                    done[h, spans[i], :] = result[i * rows : (i + 1) * rows]
-                    att_copy(h, f, targets[i], t).start()
+            for i in range(together):
+                piece_rows = result[i * count : (i + 1) * count]
+                if step + i + 1 < n_tensor:
+                    done[h, spans[i], :] = piece_rows
+                    att_copy(h, g, targets[i]).start()
                 else:
-                    mixed[f, h, :, pl.ds(pl.multiple_of(t * HS, HS), HS)] = result[
-                        i * rows : (i + 1) * rows
-                    ]
-
-    def back_far():
-        drain(mixed.at[1, :, :, pl.ds(0, (n_tensor - 1) * HS)], att_recv.at[heads])
+                    mixed[f, h, pl.ds(first, count), pl.ds(pl.multiple_of(t * HS, HS), HS)] = piece_rows
+
+    def back_far(g):
+        drain(mixed.at[1, :, pl.ds(0, part_rows), pl.ds(0, (n_tensor - 1) * HS)], att_recv.at[heads + g - 1])
 
     def back_own(h):
         drain(mixed.at[0, h, :, pl.ds(0, (n_tensor - 1) * HS)], att_recv.at[h])
@@ -347,14 +351,18 @@
         drain(weight.at[:, pl.ds(0, HS), :], far_send)
         drain(weight.at[:, pl.ds(0, 2 * HS), :], near_send)
 
-    def part_copy(p):
-        cut = cut_of(p)
-        return remote(
-            part_out.at[:, cut], part_in.at[:, cut], part_send, part_recv.at[p], device(1 - s, t, b)
-        )
-
-    def product(f, h, cut):
-        return jnp.dot(mixed[f, h], weight[h, :, cut], preferred_element_type=jnp.float32)
+    def part_copy(g, p):
+        first, count = bands[g][1:]
+        span, cut = pl.ds(first, count), cut_of(p)
+        return remote(
+            part_out.at[span, cut], part_in.at[span, cut], part_send, part_recv.at[p, g - 1], device(1 - s, t, b)
+        )
+
+    def product(g, h, cut):
+        f, first, count = bands[g]
+        return jnp.dot(
+            mixed[f, h, first : first + count], weight[h, :, cut], preferred_element_type=jnp.float32
+        )
 
     def own_product(h):
         for p in order:
@@ -364,32 +372,37 @@
     def finish(p):
         cut = cut_of(p)
         mine = own_part[:, cut] + product(0, heads - 1, cut)
-        part_copy(p).wait_recv()
+        for g in (1, 2):
+            part_copy(g, p).wait_recv()
         out_ref[0, :, cut] = (mine + part_in[:, cut].astype(jnp.float32)).astype(jnp.bfloat16)
 
-    def project_far(k):
+    def project_far(g, k):
+        first, count = bands[g][1:]
         p = order[k]
         cut = cut_of(p)
-        drain(weight.at[:, pl.ds(0, 2 * HS), cut], near_recv.at[p])
-        part_out[:, cut] = sum(product(1, h, cut) for h in range(heads)).astype(jnp.bfloat16)
-        part_copy(p).start()
-
+        if g == 1:
+            drain(weight.at[:, pl.ds(0, 2 * HS), cut], near_recv.at[p])
+        part_out[first : first + count, cut] = sum(product(g, h, cut) for h in range(heads)).astype(jnp.bfloat16)
+        part_copy(g, p).start()
+
+    def start_far(h, first, last):
+        start_kv(h, 0, first, last)
+        start_kv(h, 1, first, last)
+        start_q(h, 1, first, last)
 
     for h in range(heads):
-        start_across(h)
+        start_kv(h, 1, 0, 1)
+        start_q(h, 1, 0, 1)
+        start_q(h, 2, 0, 1)
 
     relay(1)
-    middle = ((t == 1) | (t == 2)).astype(jnp.int32)
-    inner_first = jnp.where(t == 2, 2, 1)
-    inner_last = inner_first + 2 * middle
-    outer_first = jnp.where(t == 1, 3, 1)
-    outer_last = jnp.where(t == 2, 2, 4)
+    inner = 1 + 2 * ((t == 1) | (t == 2)).astype(jnp.int32)
     for h in range(heads):
-        start_kv_far(h, inner_first, inner_last)
+        start_far(h, 1, inner)
     forward(order[0])
     relay(2)
     for h in range(heads):
-        start_kv_far(h, outer_first, outer_last)
+        start_far(h, inner, n_tensor)
     forward(order[1])
     relay(3)
 
@@ -401,20 +414,25 @@
             forward(order[2])
         if h == 1:
             forward(order[3])
-            start_own(0)
-    back_far()
-    start_own(1)
-    start_own(2)
-    project_far(0)
+            for k in range(heads):
+                start_q(k, 2, 1, n_tensor)
+    start_q(0, 0, 1, n_tensor)
+    for h in range(heads):
+        arrive_q(h, 2)
+        attend(h, 2)
+    start_q(1, 0, 1, n_tensor)
+    start_q(2, 0, 1, n_tensor)
+    back_far(1)
+    for k in range(n_tensor):
+        project_far(1, k)
     arrive_q(0, 0)
     attend(0, 0)
-    project_far(1)
-    arrive_q(1, 0)
-    attend(1, 0)
-    project_far(2)
-    arrive_q(2, 0)
-    attend(2, 0)
-    project_far(3)
+    back_far(2)
+    for k in range(n_tensor):
+        project_far(2, k)
+    for h in range(1, heads):
+        arrive_q(h, 0)
+        attend(h, 0)
     weight_sent()
     back_own(0)
     own_product(0)
@@ -453,9 +471,9 @@
             dma((2,)),
             pltpu.SemaphoreType.REGULAR((3,)),
             dma,
-            dma((heads, 3)),
-            dma,
-            dma((heads + 1,)),
+            dma((heads, 4)),
+            dma,
+            dma((heads + 2,)),
             dma,
             dma,
             dma((n_tensor, heads)),
@@ -464,7 +482,7 @@
             dma,
             dma((n_tensor,)),
             dma,
-            dma((n_tensor,)),
+            dma((n_tensor, 2)),
         ],
         compiler_params=pltpu.CompilerParams(
             collective_id=0, has_side_effects=True, vmem_limit_bytes=32 * 1024 * 1024,

time: 104 us -> 102 us (0.981)
  Pallas kernels: 103 us -> 101 us
    pallas_call x1, Pallas kernels: 103 us -> 101 us  [fused(): pl.pallas_call(functools.partial(whole_kernel, axes, sizes), out_shape=ja...]
where the time goes in v4:
time: 102 us
  Pallas kernels  101 us (99%)
    pallas_call x1, Pallas kernels, fused(): pl.pallas_call(functools.partial(whole_kernel, axes, sizes), out_shape=ja...  101 us

profile of v4, /device:TPU:0, one launch (start us, length us, event | category | flops | bytes accessed | tf_op | source)
XLA Modules:
  0.0 102.3 jit_solution(4513428294940180035)
XLA Ops:
  0.7 100.8 %shard_map.55 = bf16[1,128,3072]{2,1,0:T(8,128)(2,1)S(1)} custom-call(s32[1]{0:T(128)S(6)} %copy.7.len_ref, bf16[1,128,3072]{2,1,0:T(8,128)(2,1)} %q_ref.1, bf16[1,128,3072]{2,1,0:T(8,128)(2,1)} %k_ref.1, bf16[1,128,3072]{2,1,0:T(8,128)(2,1)} %v_ref.1, bf16[384,768]{1,0:T(8,128)(2,1)} %w_ref.1), custom_call_target="tpu_custom_call" | custom-call | tf_op jit(solution)/shard_map/pallas_call | solution.py:457
  101.5 0.9 copy.8

commit v5 on v4

--- a/solution.py
+++ b/solution.py
@@ -226,9 +226,6 @@
     def weight_load(c):
         return pltpu.make_async_copy(w_ref.at[pl.ds(c * HS, HS), :], piece(b, t, c), load_sem.at[1])
 
-    for c in range(heads):
-        weight_load(c).start()
-
     def load(j):
         return pltpu.make_async_copy(streams[j].at[0], held.at[j], load_sem.at[0])
 
@@ -253,27 +250,29 @@
             greet(semaphore, device(s, t + 1, b))
 
     beside = 1 + (t > 0).astype(jnp.int32) + (t < n_tensor - 1).astype(jnp.int32)
+    greet_group(barrier)
     greet(barrier, device(s, t, far))
     greet(barrier, device(s, t, near))
-    greet_group(barrier)
+    for c in range(heads):
+        weight_load(c).start()
+    pl.semaphore_wait(barrier, beside + 2)
+    drain(weight.at[:, pl.ds(pl.multiple_of(b * HS, HS), HS), cut_of(t)], load_sem.at[1])
+
+    for c in range(heads):
+        @pl.when(t < n_tensor - 1)
+        def _():
+            up_copy(t, c).start()
+
+        @pl.when(t > 0)
+        def _():
+            down_copy(t, c).start()
+
+        spread(t, c)
     for j in (1, 2, 0):
         load(j).start()
     for h in range(heads):
         for j in range(3):
             own_copy(h, j).start()
-    pl.semaphore_wait(barrier, beside + 2)
-    drain(weight.at[:, pl.ds(pl.multiple_of(b * HS, HS), HS), cut_of(t)], load_sem.at[1])
-
-    for c in range(heads):
-        @pl.when(t < n_tensor - 1)
-        def _():
-            up_copy(t, c).start()
-
-        @pl.when(t > 0)
-        def _():
-            down_copy(t, c).start()
-
-        spread(t, c)
     for k in range(3):
         greet_group(ready.at[k])
         pl.semaphore_wait(ready.at[k], beside)
@@ -317,7 +316,7 @@
         row = first + lax.broadcasted_iota(jnp.int32, (count, 1), 0)
         together = 2 * rows // count
         for step in range(0, n_tensor, together):
-            targets = [along(step + i + 1) for i in range(together)]
+            targets = [along(step + i + 1 if g or step + i + 1 == n_tensor else n_tensor - 1 - step - i) for i in range(together)]
             spans = [band_rows(g, side + target) for target in targets]
             result = attend_rows(
                 h,
@@ -369,12 +368,15 @@
             cut = cut_of(p)
             own_part[:, cut] = product(0, h, cut) if h == 0 else own_part[:, cut] + product(0, h, cut)
 
-    def finish(p):
+    def merge(p):
         cut = cut_of(p)
-        mine = own_part[:, cut] + product(0, heads - 1, cut)
         for g in (1, 2):
             part_copy(g, p).wait_recv()
-        out_ref[0, :, cut] = (mine + part_in[:, cut].astype(jnp.float32)).astype(jnp.bfloat16)
+        own_part[:, cut] = own_part[:, cut] + part_in[:, cut].astype(jnp.float32)
+
+    def finish(first, last):
+        cut = slice(first * w_cols, last * w_cols)
+        out_ref[0, :, cut] = (own_part[:, cut] + product(0, heads - 1, cut)).astype(jnp.bfloat16)
 
     def project_far(g, k):
         first, count = bands[g][1:]
@@ -438,9 +440,13 @@
     own_product(0)
     back_own(1)
     own_product(1)
+    for p in order:
+        merge(p)
     back_own(2)
-    for p in order:
-        finish(p)
+    finish(0, 1)
+    finish(1, 2)
+    finish(2, 3)
+    finish(3, 4)
     drain(got.at[:, :, pl.ds(0, (group - 1) * rows), :], qkv_send)
     drain(done.at[:, pl.ds(0, n_seq * (n_tensor - 1) * rows), :], att_send)
     drain(part_out, part_send)

time: 102 us -> 101 us (level)
  Pallas kernels: 101 us -> 99.6 us
    pallas_call x1, Pallas kernels: 101 us -> 99.6 us  [fused(): pl.pallas_call(functools.partial(whole_kernel, axes, sizes), out_shape=ja...]
where the time goes in v5:
time: 101 us
  Pallas kernels  99.6 us (99%)
    pallas_call x1, Pallas kernels, fused(): pl.pallas_call(functools.partial(whole_kernel, axes, sizes), out_shape=ja...  99.6 us

profile of v5, /device:TPU:0, one launch (start us, length us, event | category | flops | bytes accessed | tf_op | source)
XLA Modules:
  0.0 101.1 jit_solution(3634114175610925081)
XLA Ops:
  0.7 99.6 %shard_map.55 = bf16[1,128,3072]{2,1,0:T(8,128)(2,1)S(1)} custom-call(s32[1]{0:T(128)S(6)} %copy.7.len_ref, bf16[1,128,3072]{2,1,0:T(8,128)(2,1)} %q_ref.1, bf16[1,128,3072]{2,1,0:T(8,128)(2,1)} %k_ref.1, bf16[1,128,3072]{2,1,0:T(8,128)(2,1)} %v_ref.1, bf16[384,768]{1,0:T(8,128)(2,1)} %w_ref.1), custom_call_target="tpu_custom_call" | custom-call | tf_op jit(solution)/shard_map/pallas_call | solution.py:463
  100.2 0.9 copy.8

commit v6 on v5

--- a/solution.py
+++ b/solution.py
@@ -137,7 +137,7 @@
             held.at[j, pl.ds(first, count), cols],
             got.at[h, j, pl.ds(pl.multiple_of(me * rows + first, part_rows), count), :],
             qkv_send,
-            qkv_recv.at[h, 3 if j else g],
+            qkv_recv.at[h, 1 if j else g],
             device(ds, dt, b),
         )
 
@@ -157,7 +157,7 @@
         lax.fori_loop(first, last, body, 0)
 
     def arrive_kv(h):
-        drain(got.at[h, pl.ds(1, 2)], qkv_recv.at[h, 3])
+        drain(got.at[h, :, pl.ds(0, (2 * group * rows + n_tensor * part_rows) // 3), :], qkv_recv.at[h, 1])
 
     def arrive_q(h, g):
         drain(got.at[h, 0, pl.ds(0, n_tensor * bands[g][2]), :], qkv_recv.at[h, g])
@@ -232,7 +232,7 @@
     def own_copy(h, j):
         cols = pl.ds(pl.multiple_of((me * heads + h) * HS, HS), HS)
         return pltpu.make_async_copy(
-            streams[j].at[0, :, cols], got.at[h, j, spot(me), :], qkv_recv.at[h, 3 if j else 0]
+            streams[j].at[0, :, cols], got.at[h, j, spot(me), :], qkv_recv.at[h, 1 if j else 0]
         )
 
     def greet(semaphore, where):
@@ -354,7 +354,7 @@
         first, count = bands[g][1:]
         span, cut = pl.ds(first, count), cut_of(p)
         return remote(
-            part_out.at[span, cut], part_in.at[span, cut], part_send, part_recv.at[p, g - 1], device(1 - s, t, b)
+            part_out.at[span, cut], part_in.at[span, cut], part_send, part_recv.at[p], device(1 - s, t, b)
         )
 
     def product(g, h, cut):
@@ -370,8 +370,7 @@
 
     def merge(p):
         cut = cut_of(p)
-        for g in (1, 2):
-            part_copy(g, p).wait_recv()
+        drain(part_in.at[:, cut], part_recv.at[p])
         own_part[:, cut] = own_part[:, cut] + part_in[:, cut].astype(jnp.float32)
 
     def finish(first, last):
@@ -410,7 +409,6 @@
 
     for h in range(heads):
         arrive_kv(h)
-        arrive_q(h, 1)
         attend(h, 1)
         if h == 0:
             forward(order[2])
@@ -477,7 +475,7 @@
             dma((2,)),
             pltpu.SemaphoreType.REGULAR((3,)),
             dma,
-            dma((heads, 4)),
+            dma((heads, 3)),
             dma,
             dma((heads + 2,)),
             dma,
@@ -488,7 +486,7 @@
             dma,
             dma((n_tensor,)),
             dma,
-            dma((n_tensor, 2)),
+            dma((n_tensor,)),
         ],
         compiler_params=pltpu.CompilerParams(
             collective_id=0, has_side_effects=True, vmem_limit_bytes=32 * 1024 * 1024,

time: 101 us -> 101 us (level)
  no operation moved by 1% of the time
where the time goes in v6:
time: 101 us
  Pallas kernels  99.5 us (99%)
    pallas_call x1, Pallas kernels, fused(): pl.pallas_call(functools.partial(whole_kernel, axes, sizes), out_shape=ja...  99.5 us

profile of v6, /device:TPU:0, one launch (start us, length us, event | category | flops | bytes accessed | tf_op | source)
XLA Modules:
  0.0 101.0 jit_solution(11770585378538451984)
XLA Ops:
  0.7 99.5 %shard_map.55 = bf16[1,128,3072]{2,1,0:T(8,128)(2,1)S(1)} custom-call(s32[1]{0:T(128)S(6)} %copy.7.len_ref, bf16[1,128,3072]{2,1,0:T(8,128)(2,1)} %q_ref.1, bf16[1,128,3072]{2,1,0:T(8,128)(2,1)} %k_ref.1, bf16[1,128,3072]{2,1,0:T(8,128)(2,1)} %v_ref.1, bf16[384,768]{1,0:T(8,128)(2,1)} %w_ref.1), custom_call_target="tpu_custom_call" | custom-call | tf_op jit(solution)/shard_map/pallas_call | solution.py:461
  100.2 0.9 copy.8

commit v7 on v6

--- a/solution.py
+++ b/solution.py
@@ -397,13 +397,14 @@
         start_q(h, 2, 0, 1)
 
     relay(1)
+    held_back = 1 + 2 * ((t == 1) | (t == 2)).astype(jnp.int32) * (1 - b % 2)
     inner = 1 + 2 * ((t == 1) | (t == 2)).astype(jnp.int32)
     for h in range(heads):
-        start_far(h, 1, inner)
+        start_far(h, 1, inner if h < 2 else held_back)
     forward(order[0])
     relay(2)
     for h in range(heads):
-        start_far(h, inner, n_tensor)
+        start_far(h, inner if h < 2 else held_back, n_tensor)
     forward(order[1])
     relay(3)
 

time: 101 us -> 101 us (level)
  no operation moved by 1% of the time
where the time goes in v7:
time: 101 us
  Pallas kernels  99.5 us (99%)
    pallas_call x1, Pallas kernels, fused(): pl.pallas_call(functools.partial(whole_kernel, axes, sizes), out_shape=ja...  99.5 us

profile of v7, /device:TPU:0, one launch (start us, length us, event | category | flops | bytes accessed | tf_op | source)
XLA Modules:
  0.0 101.0 jit_solution(1149062345988366645)
XLA Ops:
  0.7 99.5 %shard_map.55 = bf16[1,128,3072]{2,1,0:T(8,128)(2,1)S(1)} custom-call(s32[1]{0:T(128)S(6)} %copy.7.len_ref, bf16[1,128,3072]{2,1,0:T(8,128)(2,1)} %q_ref.1, bf16[1,128,3072]{2,1,0:T(8,128)(2,1)} %k_ref.1, bf16[1,128,3072]{2,1,0:T(8,128)(2,1)} %v_ref.1, bf16[384,768]{1,0:T(8,128)(2,1)} %w_ref.1), custom_call_target="tpu_custom_call" | custom-call | tf_op jit(solution)/shard_map/pallas_call | solution.py:462
  100.2 0.9 copy.8
